TPU v7x, 16 devices: a 4x2x1 block of a 4x4x8 slice. The times are simulated.
16 devices in a mesh: dp: 2 (over y, z), tp: 8 (over x, core).
Axes of the slice: x: 4, y: 2, z: 1, core: 2. Of those that a mesh axis runs over, the one named last changes fastest.
The devices are a block of a 4x4x8 slice.
Arguments:
- x: bfloat16 [8192, 2048], P(('dp', 'tp')), parts along dimension 0
- w_gate: bfloat16 [2048, 8192], P(None, 'tp')
- w_up: bfloat16 [2048, 8192], P(None, 'tp')
- w_down: bfloat16 [8192, 2048], P('tp')
Outputs:
- output: bfloat16 [8192, 2048], P(('dp', 'tp')), parts along dimension 0
There are 2 independent parts. A program takes and returns all parts, laid end to end along the dimension named above; an argument that names none is the same for every part.
All inputs are finite; a program needn't handle non-finite values.
Results may differ from a plain program's by a relative error of at most 0.016.
Values are sent between devices in bfloat16 or wider.
A program may use at most 768 MiB of HBM per device.

v0:
```python
import jax
import jax.numpy as jnp
from jax import lax
from jax.sharding import PartitionSpec as P


def solution(mesh):
    def step(x, w_gate, w_up, w_down):
        rows = lax.all_gather(x, "tp", axis=0, tiled=True)
        gate = jnp.dot(rows, w_gate, preferred_element_type=jnp.float32)
        up = jnp.dot(rows, w_up, preferred_element_type=jnp.float32)
        hidden = (jax.nn.silu(gate) * up).astype(jnp.bfloat16)
        term = jnp.dot(hidden, w_down, preferred_element_type=jnp.float32).astype(jnp.bfloat16)
        return lax.psum_scatter(term, "tp", scatter_dimension=0, tiled=True)

    return jax.shard_map(
        step,
        mesh=mesh,
        in_specs=(P(("dp", "tp"), None), P(None, "tp"), P(None, "tp"), P("tp", None)),
        out_specs=P(("dp", "tp"), None),
        check_vma=False,
    )
```

profile of v0, /device:TPU:112, one launch (start us, length us, event | category | flops | bytes accessed | tf_op | source)
XLA Modules:
  0.0 264.8 jit_solution(5574834566106757697)
XLA Ops:
  6.5 0.0 all-gather.2.cloned.1.call-start
  6.6 0.7 all-gather.2.cloned.1.call-update
  7.3 0.1 reduce-scatter.2.cloned.1.call-start
  7.4 85.5 %all-gather.2.cloned.1.call-done = bf16[4096,2048]{1,0:T(8,128)(2,1)} async-done(((bf16[512,2048]{1,0:T(8,128)(2,1)}), bf16[4096,2048]{1,0:T(8,128)(2,1)}) %all-gather.2.cloned.1.call-update) | async-done | bytes 16777232 | tf_op jit(solution)/shard_map/all_gather | solution.py:9
  92.9 0.0 copy-start
  92.9 23.5 %fusion.1 = f32[4096,1024]{1,0:T(8,128)} fusion(bf16[4096,2048]{1,0:T(8,128)(2,1)} %all-gather.2.cloned.1.call-done, bf16[2048,1024]{1,0:T(8,128)(2,1)} %param.5), kind=kOutput, calls=%fused_computation.3 | convolution fusion | flops 17179869184 | bytes 37748736 | tf_op jit(solution)/shard_map/dot_general | solution.py:10
  116.4 0.0 copy-done
  116.4 0.0 copy-start.1
  116.4 29.4 %multiply_convert_fusion.clone.4 = bf16[4096,1024]{1,0:T(8,128)(2,1)} fusion(f32[4096,1024]{1,0:T(8,128)} %fusion.1, bf16[4096,2048]{1,0:T(8,128)(2,1)} %all-gather.2.cloned.1.call-done, bf16[2048,1024]{1,0:T(8,128)(2,1)S(1)} %copy-done), kind=kOutput, calls=%fused_computation.clone.clone.clone.1 | convolution fusion | flops 17205035008 | bytes 46137344 | tf_op jit(solution)/shard_map/dot_general | solution.py:11
  145.8 0.0 copy-done.1
  145.8 23.7 %convolution_convert_fusion = bf16[4096,2048]{1,0:T(8,128)(2,1)} fusion(bf16[1024,2048]{1,0:T(8,128)(2,1)S(1)} %copy-done.1, bf16[4096,1024]{1,0:T(8,128)(2,1)} %multiply_convert_fusion.clone.4), kind=kOutput, calls=%fused_computation.1 | convolution fusion | flops 17188257792 | bytes 29360128 | tf_op jit(solution)/shard_map/dot_general | solution.py:13
  169.5 0.1 reduce-scatter.2.cloned.1.call-update
  169.6 88.4 %reduce-scatter.2.cloned.1.call-done = bf16[512,2048]{1,0:T(8,128)(2,1)} async-done(((bf16[4096,2048]{1,0:T(8,128)(2,1)}), bf16[512,2048]{1,0:T(8,128)(2,1)}) %reduce-scatter.2.cloned.1.call-update) | async-done | bytes 2097168 | tf_op jit(solution)/shard_map/reduce_scatter | solution.py:14
Async XLA Ops:
  6.5 86.4 %all-gather.2.cloned.1.call-start = ((), (), s32[]{:S(2)}) async-start(), calls=%async_computation.1 | async-start | bytes 18874368 | tf_op jit(solution)/shard_map/all_gather | solution.py:9
  7.3 250.7 %reduce-scatter.2.cloned.1.call-start = ((), (), s32[]{:S(2)}) async-start(), calls=%async_computation.2 | async-start | bytes 18874368 | tf_op jit(solution)/shard_map/reduce_scatter | solution.py:14
  92.9 23.5 %copy-start = (bf16[2048,1024]{1,0:T(8,128)(2,1)S(1)}, bf16[2048,1024]{1,0:T(8,128)(2,1)}, u32[]{:S(2)}) copy-start(bf16[2048,1024]{1,0:T(8,128)(2,1)} %param.6) | copy-start | bytes 12582916
  116.4 29.4 %copy-start.1 = (bf16[1024,2048]{1,0:T(8,128)(2,1)S(1)}, bf16[1024,2048]{1,0:T(8,128)(2,1)}, u32[]{:S(2)}) copy-start(bf16[1024,2048]{1,0:T(8,128)(2,1)} %param.7) | copy-start | bytes 12582916
Sparse Core Ops, SparseCore 0:
  8.9 83.9 all-gather.1
  169.7 88.2 reduce-scatter.1
where the time goes:
time: 265 us
  waiting for transfers between devices  175 us (66%)
  matrix products  76.6 us (29%)
  between operations  13.4 us (5%)
    reduce_scatter x1, waiting for transfers between devices, step(): return lax.psum_scatter(term, 'tp', scatter_dimension=0, tiled=True)  88.4 us
    all_gather x1, waiting for transfers between devices, step(): rows = lax.all_gather(x, 'tp', axis=0, tiled=True)  85.5 us
    dot_general x1, matrix products, step(): up = jnp.dot(rows, w_up, preferred_element_type=jnp.float32)  29.4 us
    dot_general x1, matrix products, step(): jnp.dot(hidden, w_down, preferred_element_type=jnp.float32)  23.7 us
    dot_general x1, matrix products, step(): gate = jnp.dot(rows, w_gate, preferred_element_type=jnp.float32)  23.5 us
  transfers between devices with their start and end apart: 2, of which 2 were waited for; matrix products, arithmetic and copies ran while one was open for 0% of the time, Pallas kernels for 0%

commit v1 on v0

v1 whole, which is shorter than its diff:
```python
import functools

import jax
import jax.numpy as jnp
from jax import lax
from jax.experimental import pallas as pl
from jax.experimental.pallas import tpu as pltpu
from jax.sharding import PartitionSpec as P

F32 = jnp.float32
CORES = 2
PIECES = 2
ACC_PIECES = 4
TILE = 256

SLOTS = 8
STEPS = 2 * SLOTS


def kernel(
    n, x_hbm, wg_hbm, wu_hbm, wd_hbm, y_hbm,
    x_all, wg, wu, wd, hidden, acc, terms, partner_terms, arrived, staged,
    load_sem, ag_send, ag_recv, relay_send, relay_recv, pt_send, pt_recv,
    far_send, far_recv, plain_send, plain_recv, sum_send, sum_recv, out_sem,
):
    half, depth = x_all.shape[1:]
    me = lax.axis_index("tp")
    right = {"tp": lax.rem(me + CORES, n)}
    left = {"tp": lax.rem(me + n - CORES, n)}
    partner = {"tp": me + 1 - 2 * lax.rem(me, CORES)}
    part = half // PIECES
    spart = half // ACC_PIECES

    def rows(p, size):
        return pl.ds(p * size, size)

    def remote(src, dst, send, recv, device):
        return pltpu.make_async_remote_copy(
            src_ref=src, dst_ref=dst, send_sem=send, recv_sem=recv,
            device_id=device, device_id_type=pl.DeviceIdType.MESH,
        )

    def mine(slot):
        return 2 * slot + 1

    moves = [(0, 2, right), (1, 3, left), (2, 4, right), (3, 5, left), (0, 6, left), (1, 7, right)]

    def gather(m, p):
        src, dst, device = moves[m]
        return remote(
            x_all.at[mine(src), rows(p, part)], x_all.at[mine(dst), rows(p, part)],
            ag_send.at[m, p], ag_recv.at[m, p], device,
        )

    def relay(slot, p):
        return remote(
            x_all.at[mine(slot), rows(p, part)], x_all.at[2 * slot, rows(p, part)],
            relay_send.at[slot, p], relay_recv.at[slot, p], partner,
        )

    def partner_term(slot):
        return remote(
            x_all.at[2 * slot], partner_terms.at[slot], pt_send.at[slot], pt_recv.at[slot], partner
        )

    def far_term(h, p):
        return remote(
            terms.at[2 + h, rows(p, part)], arrived.at[h, rows(p, part)],
            far_send.at[h, p], far_recv.at[h, p], (right, left)[h],
        )

    def plain_term(h, p):
        return remote(
            terms.at[h, rows(p, part)], arrived.at[2 + h, rows(p, part)],
            plain_send.at[h, p], plain_recv.at[h, p], (left, right)[h],
        )

    def sum_term(h, p):
        return remote(
            terms.at[4 + h, rows(p, spart)], arrived.at[4 + h, rows(p, spart)],
            sum_send.at[h, p], sum_recv.at[h, p], (right, left)[h],
        )

    def out(h, p):
        return pltpu.make_async_copy(
            staged.at[h, rows(p, spart)], y_hbm.at[rows(h * ACC_PIECES + p, spart)], out_sem.at[h, p]
        )

    own = [pltpu.make_async_copy(x_hbm.at[rows(h, half)], x_all.at[mine(h)], load_sem.at[h]) for h in range(2)]
    weights = [
        pltpu.make_async_copy(src, dst, load_sem.at[2 + i])
        for i, (src, dst) in enumerate(((wg_hbm, wg), (wu_hbm, wu), (wd_hbm, wd)))
    ]
    for c in own + weights:
        c.start()
    barrier = pltpu.get_barrier_semaphore()
    for device in (right, left, partner):
        pl.semaphore_signal(barrier, inc=1, device_id=device, device_id_type=pl.DeviceIdType.MESH)
    pl.semaphore_wait(barrier, 3)
    for h in range(2):
        own[h].wait()
        for p in range(PIECES):
            gather(h, p).start()
    for h in range(2):
        for p in range(PIECES):
            relay(h, p).start()
    for c in weights:
        c.wait()

    def arrive(slots, p):
        for slot in slots:
            gather(slot - 2, p).wait_recv()
            if slot in (2, 3):
                gather(slot, p).start()
            relay(slot, p).start()

    def relayed(slot):
        for p in range(PIECES):
            relay(slot, p).wait_recv()

    def start_near2():
        for m in (4, 5):
            for p in range(PIECES):
                gather(m, p).start()

    before = {
        0: [lambda: relayed(0)],
        2: [lambda: relayed(1)],
        4: [lambda: arrive((2, 3), 0), lambda: arrive((2, 3), 1), start_near2, lambda: relayed(2)],
        6: [lambda: relayed(3)],
        8: [lambda: arrive((4, 5), 0), lambda: arrive((4, 5), 1), lambda: relayed(4)],
        10: [lambda: relayed(5)],
        12: [lambda: arrive((6, 7), 0), lambda: arrive((6, 7), 1), lambda: relayed(6)],
        14: [lambda: relayed(7)],
    }

    def add_rows(start, size, srcs, dst):
        chunk = 32

        @pl.loop(0, size // chunk)
        def _(i):
            r = pl.ds(pl.multiple_of(start + i * chunk, chunk), chunk)
            total = srcs[0][r, :].astype(F32)
            for s in srcs[1:]:
                total += s[r, :].astype(F32)
            dst[r, :] = total.astype(dst.dtype)

    def finish_far(h):
        partner_term(4 + h).wait_recv()
        for p in range(PIECES):
            add_rows(p * part, part, [acc.at[0], partner_terms.at[4 + h]], terms.at[2 + h])
            far_term(h, p).start()

    def finish_plain(h):
        partner_term(2 + h).wait_recv()
        add_rows(0, half, [acc.at[0], partner_terms.at[2 + h]], terms.at[h])

    def start_plain():
        for h in range(2):
            for p in range(PIECES):
                plain_term(h, p).start()

    after = {
        5: [lambda: finish_plain(0)],
        7: [lambda: finish_plain(1)],
        9: [lambda: finish_far(0)],
        11: [lambda: finish_far(1), start_plain],
    }

    def step(t, carry):
        for at, actions in before.items():

            @pl.when(t == at)
            def _():
                for a in actions:
                    a()

        rows_in = x_all.at[t]
        for c in range(0, hidden.shape[1], TILE):
            cols = pl.ds(c, TILE)
            gate = jnp.dot(rows_in[...], wg[:, cols], preferred_element_type=F32)
            up = jnp.dot(rows_in[...], wu[:, cols], preferred_element_type=F32)
            hidden[:, cols] = (jax.nn.silu(gate) * up).astype(hidden.dtype)
        slot = t // 2
        to = (t % 2) * (jnp.where(slot < 2, slot + 1, 0) + jnp.where(slot > 5, slot - 3, 0))
        for c in range(0, depth, TILE):
            cols = pl.ds(c, TILE)
            acc[to, :, cols] = jnp.dot(hidden[...], wd[:, cols], preferred_element_type=F32)

        @pl.when(t % 2 == 0)
        def _():
            add_rows(0, half, [acc.at[0]], x_all.at[t])
            partner_term(slot).start()

        for at, actions in after.items():

            @pl.when(t == at)
            def _():
                for a in actions:
                    a()

        return carry

    lax.fori_loop(0, STEPS, step, 0)

    for h in range(2):
        partner_term(6 + h).wait_recv()
    for p in range(PIECES):
        for h in range(2):
            far_term(h, p).wait_recv()
            ratio = ACC_PIECES // PIECES
            for q in range(p * ratio, (p + 1) * ratio):
                add_rows(q * spart, spart, [acc.at[3 + h], partner_terms.at[6 + h], arrived.at[h]], terms.at[4 + h])
                sum_term(h, q).start()
    for h in range(2):
        partner_term(h).wait_recv()
        for p in range(PIECES):
            plain_term(h, p).wait_recv()
        add_rows(0, half, [acc.at[1 + h], partner_terms.at[h], arrived.at[2 + h]], acc.at[1 + h])
    for p in range(ACC_PIECES):
        for h in range(2):
            sum_term(h, p).wait_recv()
            add_rows(p * spart, spart, [acc.at[1 + h], arrived.at[4 + h]], staged.at[h])
            out(h, p).start()

    for p in range(ACC_PIECES):
        for h in range(2):
            out(h, p).wait()
            sum_term(h, p).wait_send()
    for p in range(PIECES):
        for m in range(6):
            gather(m, p).wait_send()
        for slot in range(SLOTS):
            relay(slot, p).wait_send()
        for h in range(2):
            far_term(h, p).wait_send()
            plain_term(h, p).wait_send()
    for slot in range(SLOTS):
        partner_term(slot).wait_send()


def solution(mesh):
    n = mesh.shape["tp"]

    def step(x, w_gate, w_up, w_down):
        rows, depth = x.shape
        width = w_gate.shape[1]
        half = rows // 2
        dma = pltpu.SemaphoreType.DMA
        bf16 = jnp.bfloat16
        return pl.pallas_call(
            functools.partial(kernel, n),
            out_shape=jax.ShapeDtypeStruct((rows, depth), bf16),
            in_specs=[pl.BlockSpec(memory_space=pl.ANY)] * 4,
            out_specs=pl.BlockSpec(memory_space=pl.ANY),
            scratch_shapes=[
                pltpu.VMEM((STEPS, half, depth), bf16),
                pltpu.VMEM((depth, width), bf16),
                pltpu.VMEM((depth, width), bf16),
                pltpu.VMEM((width, depth), bf16),
                pltpu.VMEM((half, width), bf16),
                pltpu.VMEM((5, half, depth), F32),
                pltpu.VMEM((6, half, depth), bf16),
                pltpu.VMEM((SLOTS, half, depth), bf16),
                pltpu.VMEM((6, half, depth), bf16),
                pltpu.VMEM((2, half, depth), bf16),
                dma((5,)),
                dma((6, PIECES)),
                dma((6, PIECES)),
                dma((SLOTS, PIECES)),
                dma((SLOTS, PIECES)),
                dma((SLOTS,)),
                dma((SLOTS,)),
                dma((2, PIECES)),
                dma((2, PIECES)),
                dma((2, PIECES)),
                dma((2, PIECES)),
                dma((2, ACC_PIECES)),
                dma((2, ACC_PIECES)),
                dma((2, ACC_PIECES)),
            ],
            compiler_params=pltpu.CompilerParams(
                collective_id=0, has_side_effects=True, vmem_limit_bytes=67_000_000
            ),
        )(x, w_gate, w_up, w_down)

    return jax.shard_map(
        step,
        mesh=mesh,
        in_specs=(P(("dp", "tp"), None), P(None, "tp"), P(None, "tp"), P("tp", None)),
        out_specs=P(("dp", "tp"), None),
        check_vma=False,
    )
```

time: 265 us -> 146 us (0.55)
  waiting for transfers between devices: 175 us -> 0 us
  Pallas kernels: 0 us -> 143 us
  matrix products: 76.6 us -> 0 us
  between operations: 13.4 us -> 0.01 us
  local copies, waits for them, and re-layouts: 0.01 us -> 3.16 us
    pallas_call x0 -> x1, Pallas kernels: none -> 143 us  [step(): pl.pallas_call(functools.partial(kernel, n), out_shape=jax.ShapeDtypeStru...]
    reduce_scatter x1 -> x0, waiting for transfers between devices: 88.4 us -> none  [step(): return lax.psum_scatter(term, 'tp', scatter_dimension=0, tiled=True)]
    all_gather x1 -> x0, waiting for transfers between devices: 85.5 us -> none  [step(): rows = lax.all_gather(x, 'tp', axis=0, tiled=True)]
    dot_general x3 -> x0, matrix products: 76.6 us -> none  [the longest x1 29.4 us: step(): up = jnp.dot(rows, w_up, preferred_element_type=jnp.float32)]
    unnamed x4 -> x1, local copies, waits for them, and re-layouts: 0.01 us -> 3.16 us
  transfers between devices with their start and end apart: 2 -> 0, of which waited for: 2 -> 0; matrix products, arithmetic and copies ran while one was open for 0% -> 0% of each run, Pallas kernels for 0% -> 0%
where the time goes in v1:
time: 146 us
  Pallas kernels  143 us (98%)
  local copies, waits for them, and re-layouts  3.16 us (2%)
    pallas_call x1, Pallas kernels, step(): pl.pallas_call(functools.partial(kernel, n), out_shape=jax.ShapeDtypeStru...  143 us
    unnamed x1, local copies, waits for them, and re-layouts  3.16 us

profile of v1, /device:TPU:112, one launch (start us, length us, event | category | flops | bytes accessed | tf_op | source)
XLA Modules:
  0.0 145.8 jit_solution(16996846121376110364)
XLA Ops:
  0.0 142.7 %shard_map.46 = bf16[512,2048]{1,0:T(8,128)(2,1)} custom-call(bf16[512,2048]{1,0:T(8,128)(2,1)} %x_hbm.1, bf16[2048,1024]{1,0:T(8,128)(2,1)} %wg_hbm.1, bf16[2048,1024]{1,0:T(8,128)(2,1)} %wu_hbm.1, bf16[1024,2048]{1,0:T(8,128)(2,1)} %wd_hbm.1), custom_call_target="tpu_custom_call" | custom-call | tf_op jit(solution)/shard_map/pallas_call | solution.py:251
  142.7 3.2 %copy.6 = bf16[512,2048]{1,0:T(8,128)(2,1)} copy(bf16[512,2048]{1,0:T(8,128)(2,1)} %shard_map.46) | data formatting | bytes 4194304

commit v2 on v1

--- a/solution.py
+++ b/solution.py
@@ -18,10 +18,10 @@
 
 
 def kernel(
-    n, x_hbm, wg_hbm, wu_hbm, wd_hbm, y_hbm,
-    x_all, wg, wu, wd, hidden, acc, terms, partner_terms, arrived, staged,
+    n, x_hbm, wg_hbm, wu_hbm, wd_hbm, y_ref,
+    x_all, wg, wu, wd, hidden, acc, terms, partner_terms, arrived,
     load_sem, ag_send, ag_recv, relay_send, relay_recv, pt_send, pt_recv,
-    far_send, far_recv, plain_send, plain_recv, sum_send, sum_recv, out_sem,
+    far_send, far_recv, plain_send, plain_recv, sum_send, sum_recv,
 ):
     half, depth = x_all.shape[1:]
     me = lax.axis_index("tp")
@@ -79,11 +79,6 @@
         return remote(
             terms.at[4 + h, rows(p, spart)], arrived.at[4 + h, rows(p, spart)],
             sum_send.at[h, p], sum_recv.at[h, p], (right, left)[h],
-        )
-
-    def out(h, p):
-        return pltpu.make_async_copy(
-            staged.at[h, rows(p, spart)], y_hbm.at[rows(h * ACC_PIECES + p, spart)], out_sem.at[h, p]
         )
 
     own = [pltpu.make_async_copy(x_hbm.at[rows(h, half)], x_all.at[mine(h)], load_sem.at[h]) for h in range(2)]
@@ -220,12 +215,10 @@
     for p in range(ACC_PIECES):
         for h in range(2):
             sum_term(h, p).wait_recv()
-            add_rows(p * spart, spart, [acc.at[1 + h], arrived.at[4 + h]], staged.at[h])
-            out(h, p).start()
+            add_rows(p * spart, spart, [acc.at[1 + h], arrived.at[4 + h]], y_ref.at[pl.ds(h * half, half)])
 
     for p in range(ACC_PIECES):
         for h in range(2):
-            out(h, p).wait()
             sum_term(h, p).wait_send()
     for p in range(PIECES):
         for m in range(6):
@@ -250,9 +243,9 @@
         bf16 = jnp.bfloat16
         return pl.pallas_call(
             functools.partial(kernel, n),
-            out_shape=jax.ShapeDtypeStruct((rows, depth), bf16),
+            out_shape=pltpu.VMEM((rows, depth), bf16),
             in_specs=[pl.BlockSpec(memory_space=pl.ANY)] * 4,
-            out_specs=pl.BlockSpec(memory_space=pl.ANY),
+            out_specs=pl.BlockSpec(memory_space=pltpu.VMEM),
             scratch_shapes=[
                 pltpu.VMEM((STEPS, half, depth), bf16),
                 pltpu.VMEM((depth, width), bf16),
@@ -263,7 +256,6 @@
                 pltpu.VMEM((6, half, depth), bf16),
                 pltpu.VMEM((SLOTS, half, depth), bf16),
                 pltpu.VMEM((6, half, depth), bf16),
-                pltpu.VMEM((2, half, depth), bf16),
                 dma((5,)),
                 dma((6, PIECES)),
                 dma((6, PIECES)),
@@ -277,10 +269,9 @@
                 dma((2, PIECES)),
                 dma((2, ACC_PIECES)),
                 dma((2, ACC_PIECES)),
-                dma((2, ACC_PIECES)),
             ],
             compiler_params=pltpu.CompilerParams(
-                collective_id=0, has_side_effects=True, vmem_limit_bytes=67_000_000
+                collective_id=0, has_side_effects=True, vmem_limit_bytes=61 * 2**20
             ),
         )(x, w_gate, w_up, w_down)
 

time: 146 us -> 143 us (0.979)
  local copies, waits for them, and re-layouts: 3.16 us -> 1.32 us
    unnamed x1, local copies, waits for them, and re-layouts: 3.16 us -> 1.32 us
where the time goes in v2:
time: 143 us
  Pallas kernels  142 us (99%)
    pallas_call x1, Pallas kernels, step(): pl.pallas_call(functools.partial(kernel, n), out_shape=pltpu.VMEM((rows,...  142 us

profile of v2, /device:TPU:112, one launch (start us, length us, event | category | flops | bytes accessed | tf_op | source)
XLA Modules:
  0.0 143.2 jit_solution(3395859557372734099)
XLA Ops:
  0.0 141.8 %shard_map.46 = bf16[512,2048]{1,0:T(8,128)(2,1)S(1)} custom-call(bf16[512,2048]{1,0:T(8,128)(2,1)} %x_hbm.1, bf16[2048,1024]{1,0:T(8,128)(2,1)} %wg_hbm.1, bf16[2048,1024]{1,0:T(8,128)(2,1)} %wu_hbm.1, bf16[1024,2048]{1,0:T(8,128)(2,1)} %wd_hbm.1), custom_call_target="tpu_custom_call" | custom-call | tf_op jit(solution)/shard_map/pallas_call | solution.py:244
  141.9 1.3 copy.6

commit v3 on v2

v3 whole, which is shorter than its diff:
```python
import functools

import jax
import jax.numpy as jnp
from jax import lax
from jax.experimental import pallas as pl
from jax.experimental.pallas import tpu as pltpu
from jax.sharding import PartitionSpec as P

F32 = jnp.float32
CORES = 2
PIECES = 2
LAST = 32
TILE = 256

SLOTS = 8
STEPS = 2 * SLOTS


def kernel(
    n, x_hbm, wg_hbm, wu_hbm, wd_hbm, y_ref,
    x_all, wg, wu, wd, hidden, acc, terms, partner_terms, arrived,
    own_sem, weight_sem, ring_send, partner_send, near_recv, half_recv, relay_recv, pt_recv,
    far_recv, plain_recv, sum_recv,
):
    half, depth = x_all.shape[1:]
    me = lax.axis_index("tp")
    right = {"tp": lax.rem(me + CORES, n)}
    left = {"tp": lax.rem(me + n - CORES, n)}
    partner = {"tp": me + 1 - 2 * lax.rem(me, CORES)}
    part = half // PIECES
    pieces = [pl.ds(p * part, part) for p in range(PIECES)]
    whole = pl.ds(0, half)
    sums = [(0, part), (part, half - part - LAST), (half - LAST, LAST)]

    def remote(src, dst, send, recv, device):
        return pltpu.make_async_remote_copy(
            src_ref=src, dst_ref=dst, send_sem=send, recv_sem=recv,
            device_id=device, device_id_type=pl.DeviceIdType.MESH,
        )

    def mine(slot):
        return 2 * slot + 1

    moves = [(0, right), (1, left), (2, right), (3, left), (0, left), (1, right)]

    def gather(slot, p=None):
        src, device = moves[slot - 2]
        rows = whole if p is None else pieces[p]
        recv = near_recv.at[slot - 2, p] if slot < 4 else half_recv.at[slot - 4]
        return remote(
            x_all.at[mine(src), rows], x_all.at[mine(slot), rows], ring_send.at[0], recv, device
        )

    def relay(slot, rows=whole):
        return remote(
            x_all.at[mine(slot), rows], x_all.at[2 * slot, rows],
            partner_send.at[0], relay_recv.at[slot % 2], partner,
        )

    def partner_term(slot):
        return remote(
            x_all.at[2 * slot], partner_terms.at[slot], partner_send.at[0], pt_recv.at[slot % 2], partner
        )

    def far_term(h, p):
        return remote(
            terms.at[2 + h, pieces[p]], arrived.at[h, pieces[p]],
            ring_send.at[0], far_recv.at[h, p], (right, left)[h],
        )

    def plain_term(h):
        return remote(
            terms.at[h], arrived.at[2 + h], ring_send.at[0], plain_recv.at[h], (left, right)[h]
        )

    def sum_term(h, p):
        rows = pl.ds(*sums[p])
        return remote(
            terms.at[4 + h, rows], arrived.at[4 + h, rows],
            ring_send.at[0], sum_recv.at[h, p], (right, left)[h],
        )

    own = [pltpu.make_async_copy(x_hbm.at[pl.ds(h * half, half)], x_all.at[mine(h)], own_sem.at[h]) for h in range(2)]
    weights = [
        pltpu.make_async_copy(src, dst, weight_sem.at[i])
        for i, (src, dst) in enumerate(((wg_hbm, wg), (wu_hbm, wu), (wd_hbm, wd)))
    ]
    for c in own:
        c.start()
    barrier = pltpu.get_barrier_semaphore()
    for device in (right, left, partner):
        pl.semaphore_signal(barrier, inc=1, device_id=device, device_id_type=pl.DeviceIdType.MESH)
    pl.semaphore_wait(barrier, 3)
    for h in range(2):
        own[h].wait()
        for p in range(PIECES):
            gather(2 + h, p).start()
    for c in weights:
        c.start()
    for h in range(2):
        relay(h).start()
    for c in weights:
        c.wait()

    def arrive_near(p):
        for slot in (2, 3):
            gather(slot, p).wait_recv()
            gather(slot + 2, p).start()
            relay(slot, pieces[p]).start()

    def arrive_half(slots):
        for slot in slots:
            gather(slot).wait_recv()
            relay(slot).start()

    def relayed(slot):
        relay(slot).wait_recv()

    def start_near2():
        for slot in (6, 7):
            gather(slot).start()

    def own_terms():
        for h in range(2):
            partner_term(h).wait_recv()

    before = {
        0: [lambda: relayed(0)],
        2: [lambda: relayed(1)],
        4: [own_terms, lambda: arrive_near(0), lambda: arrive_near(1), start_near2, lambda: relayed(2)],
        6: [lambda: relayed(3)],
        8: [lambda: arrive_half((4, 5)), lambda: relayed(4)],
        10: [lambda: relayed(5)],
        12: [lambda: arrive_half((6, 7)), lambda: relayed(6)],
        14: [lambda: relayed(7)],
    }

    def add_rows(start, size, srcs, dst):
        chunk = 32

        @pl.loop(0, size // chunk)
        def _(i):
            r = pl.ds(pl.multiple_of(start + i * chunk, chunk), chunk)
            total = srcs[0][r, :].astype(F32)
            for s in srcs[1:]:
                total += s[r, :].astype(F32)
            dst[r, :] = total.astype(dst.dtype)

    def finish_far(h):
        partner_term(4 + h).wait_recv()
        for p in range(PIECES):
            add_rows(p * part, part, [acc.at[0], partner_terms.at[4 + h]], terms.at[2 + h])
            far_term(h, p).start()

    def finish_plain(h):
        partner_term(2 + h).wait_recv()
        add_rows(0, half, [acc.at[0], partner_terms.at[2 + h]], terms.at[h])

    def start_plain():
        for h in range(2):
            plain_term(h).start()

    after = {
        5: [lambda: finish_plain(0)],
        7: [lambda: finish_plain(1)],
        9: [lambda: finish_far(0)],
        11: [lambda: finish_far(1), start_plain],
    }

    def step(t, carry):
        for at, actions in before.items():

            @pl.when(t == at)
            def _():
                for a in actions:
                    a()

        rows_in = x_all.at[t]
        for c in range(0, hidden.shape[1], TILE):
            cols = pl.ds(c, TILE)
            gate = jnp.dot(rows_in[...], wg[:, cols], preferred_element_type=F32)
            up = jnp.dot(rows_in[...], wu[:, cols], preferred_element_type=F32)
            hidden[:, cols] = (jax.nn.silu(gate) * up).astype(hidden.dtype)
        slot = t // 2
        to = (t % 2) * (jnp.where(slot < 2, slot + 1, 0) + jnp.where(slot > 5, slot - 3, 0))
        for c in range(0, depth, TILE):
            cols = pl.ds(c, TILE)
            acc[to, :, cols] = jnp.dot(hidden[...], wd[:, cols], preferred_element_type=F32)

        @pl.when(t % 2 == 0)
        def _():
            add_rows(0, half, [acc.at[0]], x_all.at[t])
            remote(
                x_all.at[t], partner_terms.at[slot], partner_send.at[0], pt_recv.at[slot % 2], partner
            ).start()

        for at, actions in after.items():

            @pl.when(t == at)
            def _():
                for a in actions:
                    a()

        return carry

    lax.fori_loop(0, STEPS, step, 0)

    for h in range(2):
        partner_term(6 + h).wait_recv()
    for p in range(PIECES):
        for h in range(2):
            far_term(h, p).wait_recv()
            for q in ((0,), (1, 2))[p]:
                add_rows(*sums[q], [acc.at[3 + h], partner_terms.at[6 + h], arrived.at[h]], terms.at[4 + h])
                sum_term(h, q).start()
    for h in range(2):
        plain_term(h).wait_recv()
        add_rows(0, half, [acc.at[1 + h], partner_terms.at[h], arrived.at[2 + h]], acc.at[1 + h])
    pltpu.make_async_copy(x_all, x_all, partner_send.at[0]).wait()
    for p in range(len(sums)):
        for h in range(2):
            sum_term(h, p).wait_recv()
            add_rows(*sums[p], [acc.at[1 + h], arrived.at[4 + h]], y_ref.at[pl.ds(h * half, half)])
    sent = x_all.at[pl.ds(0, 12)]
    pltpu.make_async_copy(sent, sent, ring_send.at[0]).wait()


def solution(mesh):
    n = mesh.shape["tp"]

    def step(x, w_gate, w_up, w_down):
        rows, depth = x.shape
        width = w_gate.shape[1]
        half = rows // 2
        dma = pltpu.SemaphoreType.DMA
        bf16 = jnp.bfloat16
        return pl.pallas_call(
            functools.partial(kernel, n),
            out_shape=pltpu.VMEM((rows, depth), bf16),
            in_specs=[pl.BlockSpec(memory_space=pl.ANY)] * 4,
            out_specs=pl.BlockSpec(memory_space=pltpu.VMEM),
            scratch_shapes=[
                pltpu.VMEM((STEPS, half, depth), bf16),
                pltpu.VMEM((depth, width), bf16),
                pltpu.VMEM((depth, width), bf16),
                pltpu.VMEM((width, depth), bf16),
                pltpu.VMEM((half, width), bf16),
                pltpu.VMEM((5, half, depth), F32),
                pltpu.VMEM((6, half, depth), bf16),
                pltpu.VMEM((SLOTS, half, depth), bf16),
                pltpu.VMEM((6, half, depth), bf16),
                dma((2,)),
                dma((3,)),
                dma((1,)),
                dma((1,)),
                dma((2, PIECES)),
                dma((4,)),
                dma((2,)),
                dma((2,)),
                dma((2, PIECES)),
                dma((2,)),
                dma((2, 3)),
            ],
            compiler_params=pltpu.CompilerParams(
                collective_id=0, has_side_effects=True, vmem_limit_bytes=61 * 2**20
            ),
        )(x, w_gate, w_up, w_down)

    return jax.shard_map(
        step,
        mesh=mesh,
        in_specs=(P(("dp", "tp"), None), P(None, "tp"), P(None, "tp"), P("tp", None)),
        out_specs=P(("dp", "tp"), None),
        check_vma=False,
    )
```

time: 143 us -> 142 us (level)
  no operation moved by 1% of the time
where the time goes in v3:
time: 142 us
  Pallas kernels  141 us (99%)
    pallas_call x1, Pallas kernels, step(): pl.pallas_call(functools.partial(kernel, n), out_shape=pltpu.VMEM((rows,...  141 us

profile of v3, /device:TPU:112, one launch (start us, length us, event | category | flops | bytes accessed | tf_op | source)
XLA Modules:
  0.0 142.3 jit_solution(11211878396479434600)
XLA Ops:
  0.0 141.0 %shard_map.46 = bf16[512,2048]{1,0:T(8,128)(2,1)S(1)} custom-call(bf16[512,2048]{1,0:T(8,128)(2,1)} %x_hbm.1, bf16[2048,1024]{1,0:T(8,128)(2,1)} %wg_hbm.1, bf16[2048,1024]{1,0:T(8,128)(2,1)} %wu_hbm.1, bf16[1024,2048]{1,0:T(8,128)(2,1)} %wd_hbm.1), custom_call_target="tpu_custom_call" | custom-call | tf_op jit(solution)/shard_map/pallas_call | solution.py:238
  141.0 1.3 copy.6

commit v4 on v3

--- a/solution.py
+++ b/solution.py
@@ -10,6 +10,7 @@
 F32 = jnp.float32
 CORES = 2
 PIECES = 2
+FIRST = 64
 LAST = 32
 TILE = 256
 
@@ -21,7 +22,7 @@
     n, x_hbm, wg_hbm, wu_hbm, wd_hbm, y_ref,
     x_all, wg, wu, wd, hidden, acc, terms, partner_terms, arrived,
     own_sem, weight_sem, ring_send, partner_send, near_recv, half_recv, relay_recv, pt_recv,
-    far_recv, plain_recv, sum_recv,
+    sum_recv,
 ):
     half, depth = x_all.shape[1:]
     me = lax.axis_index("tp")
@@ -30,8 +31,9 @@
     partner = {"tp": me + 1 - 2 * lax.rem(me, CORES)}
     part = half // PIECES
     pieces = [pl.ds(p * part, part) for p in range(PIECES)]
+    near = [(0, FIRST), (FIRST, half - FIRST)]
     whole = pl.ds(0, half)
-    sums = [(0, part), (part, half - part - LAST), (half - LAST, LAST)]
+    sums = [(0, half - LAST), (half - LAST, LAST)]
 
     def remote(src, dst, send, recv, device):
         return pltpu.make_async_remote_copy(
@@ -46,7 +48,7 @@
 
     def gather(slot, p=None):
         src, device = moves[slot - 2]
-        rows = whole if p is None else pieces[p]
+        rows = whole if p is None else pl.ds(*near[p])
         recv = near_recv.at[slot - 2, p] if slot < 4 else half_recv.at[slot - 4]
         return remote(
             x_all.at[mine(src), rows], x_all.at[mine(slot), rows], ring_send.at[0], recv, device
@@ -66,25 +68,31 @@
     def far_term(h, p):
         return remote(
             terms.at[2 + h, pieces[p]], arrived.at[h, pieces[p]],
-            ring_send.at[0], far_recv.at[h, p], (right, left)[h],
+            ring_send.at[0], near_recv.at[1 - h, p], (right, left)[h],
         )
 
     def plain_term(h):
         return remote(
-            terms.at[h], arrived.at[2 + h], ring_send.at[0], plain_recv.at[h], (left, right)[h]
+            terms.at[h], arrived.at[2 + h], ring_send.at[0], own_sem.at[h, 0], (left, right)[h]
         )
 
     def sum_term(h, p):
         rows = pl.ds(*sums[p])
-        return remote(
-            terms.at[4 + h, rows], arrived.at[4 + h, rows],
-            ring_send.at[0], sum_recv.at[h, p], (right, left)[h],
-        )
-
-    own = [pltpu.make_async_copy(x_hbm.at[pl.ds(h * half, half)], x_all.at[mine(h)], own_sem.at[h]) for h in range(2)]
+        recv = half_recv.at[h] if p == 0 else sum_recv.at[h]
+        return remote(
+            terms.at[4 + h, rows], arrived.at[4 + h, rows], ring_send.at[0], recv, (right, left)[h]
+        )
+
+    own = [
+        pltpu.make_async_copy(
+            x_hbm.at[pl.ds(h * half + start, size)], x_all.at[mine(h), pl.ds(start, size)], own_sem.at[h, p]
+        )
+        for p, (start, size) in enumerate(near)
+        for h in range(2)
+    ]
     weights = [
-        pltpu.make_async_copy(src, dst, weight_sem.at[i])
-        for i, (src, dst) in enumerate(((wg_hbm, wg), (wu_hbm, wu), (wd_hbm, wd)))
+        pltpu.make_async_copy(src, dst, weight_sem.at[0])
+        for src, dst in ((wg_hbm, wg), (wu_hbm, wu), (wd_hbm, wd))
     ]
     for c in own:
         c.start()
@@ -92,22 +100,24 @@
     for device in (right, left, partner):
         pl.semaphore_signal(barrier, inc=1, device_id=device, device_id_type=pl.DeviceIdType.MESH)
     pl.semaphore_wait(barrier, 3)
-    for h in range(2):
-        own[h].wait()
-        for p in range(PIECES):
+    for p in range(len(near)):
+        for h in range(2):
+            own[2 * p + h].wait()
             gather(2 + h, p).start()
     for c in weights:
         c.start()
     for h in range(2):
         relay(h).start()
-    for c in weights:
-        c.wait()
+    blocks = 3 * wg.shape[1] // half
+    assert wd.shape == wg.shape[::-1] and blocks <= STEPS
+    loaded = x_all.at[pl.ds(0, blocks)]
+    pltpu.make_async_copy(loaded, loaded, weight_sem.at[0]).wait()
 
     def arrive_near(p):
         for slot in (2, 3):
             gather(slot, p).wait_recv()
             gather(slot + 2, p).start()
-            relay(slot, pieces[p]).start()
+            relay(slot, pl.ds(*near[p])).start()
 
     def arrive_half(slots):
         for slot in slots:
@@ -211,9 +221,10 @@
     for p in range(PIECES):
         for h in range(2):
             far_term(h, p).wait_recv()
-            for q in ((0,), (1, 2))[p]:
-                add_rows(*sums[q], [acc.at[3 + h], partner_terms.at[6 + h], arrived.at[h]], terms.at[4 + h])
-                sum_term(h, q).start()
+    for q in range(len(sums)):
+        for h in range(2):
+            add_rows(*sums[q], [acc.at[3 + h], partner_terms.at[6 + h], arrived.at[h]], terms.at[4 + h])
+            sum_term(h, q).start()
     for h in range(2):
         plain_term(h).wait_recv()
         add_rows(0, half, [acc.at[1 + h], partner_terms.at[h], arrived.at[2 + h]], acc.at[1 + h])
@@ -250,17 +261,15 @@
                 pltpu.VMEM((6, half, depth), bf16),
                 pltpu.VMEM((SLOTS, half, depth), bf16),
                 pltpu.VMEM((6, half, depth), bf16),
-                dma((2,)),
-                dma((3,)),
+                dma((2, 2)),
+                dma((1,)),
                 dma((1,)),
                 dma((1,)),
                 dma((2, PIECES)),
                 dma((4,)),
                 dma((2,)),
                 dma((2,)),
-                dma((2, PIECES)),
                 dma((2,)),
-                dma((2, 3)),
             ],
             compiler_params=pltpu.CompilerParams(
                 collective_id=0, has_side_effects=True, vmem_limit_bytes=61 * 2**20

time: 142 us -> 142 us (level)
  no operation moved by 1% of the time
where the time goes in v4:
time: 142 us
  Pallas kernels  141 us (99%)
    pallas_call x1, Pallas kernels, step(): pl.pallas_call(functools.partial(kernel, n), out_shape=pltpu.VMEM((rows,...  141 us

profile of v4, /device:TPU:112, one launch (start us, length us, event | category | flops | bytes accessed | tf_op | source)
XLA Modules:
  0.0 142.0 jit_solution(4729562121959199717)
XLA Ops:
  0.0 140.6 %shard_map.46 = bf16[512,2048]{1,0:T(8,128)(2,1)S(1)} custom-call(bf16[512,2048]{1,0:T(8,128)(2,1)} %x_hbm.1, bf16[2048,1024]{1,0:T(8,128)(2,1)} %wg_hbm.1, bf16[2048,1024]{1,0:T(8,128)(2,1)} %wu_hbm.1, bf16[1024,2048]{1,0:T(8,128)(2,1)} %wd_hbm.1), custom_call_target="tpu_custom_call" | custom-call | tf_op jit(solution)/shard_map/pallas_call | solution.py:249
  140.7 1.3 copy.6

commit v5 on v4

--- a/solution.py
+++ b/solution.py
@@ -10,7 +10,7 @@
 F32 = jnp.float32
 CORES = 2
 PIECES = 2
-FIRST = 64
+FIRST = 32
 LAST = 32
 TILE = 256
 
@@ -22,7 +22,6 @@
     n, x_hbm, wg_hbm, wu_hbm, wd_hbm, y_ref,
     x_all, wg, wu, wd, hidden, acc, terms, partner_terms, arrived,
     own_sem, weight_sem, ring_send, partner_send, near_recv, half_recv, relay_recv, pt_recv,
-    sum_recv,
 ):
     half, depth = x_all.shape[1:]
     me = lax.axis_index("tp")
@@ -49,7 +48,7 @@
     def gather(slot, p=None):
         src, device = moves[slot - 2]
         rows = whole if p is None else pl.ds(*near[p])
-        recv = near_recv.at[slot - 2, p] if slot < 4 else half_recv.at[slot - 4]
+        recv = near_recv.at[slot - 2, p] if slot < 4 else half_recv.at[slot - 4] if slot < 6 else own_sem.at[slot - 6, 0]
         return remote(
             x_all.at[mine(src), rows], x_all.at[mine(slot), rows], ring_send.at[0], recv, device
         )
@@ -65,20 +64,19 @@
             x_all.at[2 * slot], partner_terms.at[slot], partner_send.at[0], pt_recv.at[slot % 2], partner
         )
 
-    def far_term(h, p):
-        return remote(
-            terms.at[2 + h, pieces[p]], arrived.at[h, pieces[p]],
-            ring_send.at[0], near_recv.at[1 - h, p], (right, left)[h],
+    def far_term(h, rows=whole):
+        return remote(
+            terms.at[2 + h, rows], arrived.at[h, rows], ring_send.at[0], near_recv.at[1 - h, 0], (right, left)[h]
         )
 
     def plain_term(h):
         return remote(
-            terms.at[h], arrived.at[2 + h], ring_send.at[0], own_sem.at[h, 0], (left, right)[h]
+            terms.at[h], arrived.at[2 + h], ring_send.at[0], near_recv.at[h, 1], (left, right)[h]
         )
 
     def sum_term(h, p):
         rows = pl.ds(*sums[p])
-        recv = half_recv.at[h] if p == 0 else sum_recv.at[h]
+        recv = half_recv.at[h] if p == 0 else own_sem.at[h, 1]
         return remote(
             terms.at[4 + h, rows], arrived.at[4 + h, rows], ring_send.at[0], recv, (right, left)[h]
         )
@@ -94,7 +92,7 @@
         pltpu.make_async_copy(src, dst, weight_sem.at[0])
         for src, dst in ((wg_hbm, wg), (wu_hbm, wu), (wd_hbm, wd))
     ]
-    for c in own:
+    for c in own + weights:
         c.start()
     barrier = pltpu.get_barrier_semaphore()
     for device in (right, left, partner):
@@ -104,15 +102,8 @@
         for h in range(2):
             own[2 * p + h].wait()
             gather(2 + h, p).start()
-    for c in weights:
-        c.start()
     for h in range(2):
         relay(h).start()
-    blocks = 3 * wg.shape[1] // half
-    assert wd.shape == wg.shape[::-1] and blocks <= STEPS
-    loaded = x_all.at[pl.ds(0, blocks)]
-    pltpu.make_async_copy(loaded, loaded, weight_sem.at[0]).wait()
-
     def arrive_near(p):
         for slot in (2, 3):
             gather(slot, p).wait_recv()
@@ -124,6 +115,13 @@
             gather(slot).wait_recv()
             relay(slot).start()
 
+    blocks = 3 * wg.shape[1] // half
+    assert wd.shape == wg.shape[::-1] and blocks <= STEPS
+    loaded = x_all.at[pl.ds(0, blocks)]
+
+    def have_weights():
+        pltpu.make_async_copy(loaded, loaded, weight_sem.at[0]).wait()
+
     def relayed(slot):
         relay(slot).wait_recv()
 
@@ -136,7 +134,7 @@
             partner_term(h).wait_recv()
 
     before = {
-        0: [lambda: relayed(0)],
+        0: [lambda: relayed(0), have_weights],
         2: [lambda: relayed(1)],
         4: [own_terms, lambda: arrive_near(0), lambda: arrive_near(1), start_near2, lambda: relayed(2)],
         6: [lambda: relayed(3)],
@@ -161,7 +159,7 @@
         partner_term(4 + h).wait_recv()
         for p in range(PIECES):
             add_rows(p * part, part, [acc.at[0], partner_terms.at[4 + h]], terms.at[2 + h])
-            far_term(h, p).start()
+            far_term(h, pieces[p]).start()
 
     def finish_plain(h):
         partner_term(2 + h).wait_recv()
@@ -218,9 +216,8 @@
 
     for h in range(2):
         partner_term(6 + h).wait_recv()
-    for p in range(PIECES):
-        for h in range(2):
-            far_term(h, p).wait_recv()
+    for h in range(2):
+        far_term(h).wait_recv()
     for q in range(len(sums)):
         for h in range(2):
             add_rows(*sums[q], [acc.at[3 + h], partner_terms.at[6 + h], arrived.at[h]], terms.at[4 + h])
@@ -266,7 +263,6 @@
                 dma((1,)),
                 dma((1,)),
                 dma((2, PIECES)),
-                dma((4,)),
                 dma((2,)),
                 dma((2,)),
                 dma((2,)),

time: 142 us -> 142 us (level)
  no operation moved by 1% of the time
where the time goes in v5:
time: 142 us
  Pallas kernels  141 us (99%)
    pallas_call x1, Pallas kernels, step(): pl.pallas_call(functools.partial(kernel, n), out_shape=pltpu.VMEM((rows,...  141 us

profile of v5, /device:TPU:112, one launch (start us, length us, event | category | flops | bytes accessed | tf_op | source)
XLA Modules:
  0.0 141.9 jit_solution(9580785464493202887)
XLA Ops:
  0.0 140.6 %shard_map.46 = bf16[512,2048]{1,0:T(8,128)(2,1)S(1)} custom-call(bf16[512,2048]{1,0:T(8,128)(2,1)} %x_hbm.1, bf16[2048,1024]{1,0:T(8,128)(2,1)} %wg_hbm.1, bf16[2048,1024]{1,0:T(8,128)(2,1)} %wu_hbm.1, bf16[1024,2048]{1,0:T(8,128)(2,1)} %wd_hbm.1), custom_call_target="tpu_custom_call" | custom-call | tf_op jit(solution)/shard_map/pallas_call | solution.py:246
  140.6 1.3 copy.6

commit v6 on v5

--- a/solution.py
+++ b/solution.py
@@ -10,7 +10,7 @@
 F32 = jnp.float32
 CORES = 2
 PIECES = 2
-FIRST = 32
+FIRST = 64
 LAST = 32
 TILE = 256
 
@@ -45,13 +45,12 @@
 
     moves = [(0, right), (1, left), (2, right), (3, left), (0, left), (1, right)]
 
-    def gather(slot, p=None):
+    def gather(slot, p=None, start=None):
         src, device = moves[slot - 2]
         rows = whole if p is None else pl.ds(*near[p])
         recv = near_recv.at[slot - 2, p] if slot < 4 else half_recv.at[slot - 4] if slot < 6 else own_sem.at[slot - 6, 0]
-        return remote(
-            x_all.at[mine(src), rows], x_all.at[mine(slot), rows], ring_send.at[0], recv, device
-        )
+        origin = x_all.at[mine(src), rows] if start is None else start
+        return remote(origin, x_all.at[mine(slot), rows], ring_send.at[0], recv, device)
 
     def relay(slot, rows=whole):
         return remote(
@@ -92,16 +91,19 @@
         pltpu.make_async_copy(src, dst, weight_sem.at[0])
         for src, dst in ((wg_hbm, wg), (wu_hbm, wu), (wd_hbm, wd))
     ]
+    barrier = pltpu.get_barrier_semaphore()
+    for device in (partner, right, left):
+        pl.semaphore_signal(barrier, inc=1, device_id=device, device_id_type=pl.DeviceIdType.MESH)
     for c in own + weights:
         c.start()
-    barrier = pltpu.get_barrier_semaphore()
-    for device in (right, left, partner):
-        pl.semaphore_signal(barrier, inc=1, device_id=device, device_id_type=pl.DeviceIdType.MESH)
     pl.semaphore_wait(barrier, 3)
-    for p in range(len(near)):
-        for h in range(2):
-            own[2 * p + h].wait()
-            gather(2 + h, p).start()
+    for h in range(2):
+        gather(2 + h, 0, x_hbm.at[pl.ds(h * half, FIRST)]).start()
+    for h in range(2):
+        own[h].wait()
+    for h in range(2):
+        own[2 + h].wait()
+        gather(2 + h, 1).start()
     for h in range(2):
         relay(h).start()
     def arrive_near(p):

time: 142 us -> 142 us (level)
  no operation moved by 1% of the time
where the time goes in v6:
time: 142 us
  Pallas kernels  140 us (99%)
    pallas_call x1, Pallas kernels, step(): pl.pallas_call(functools.partial(kernel, n), out_shape=pltpu.VMEM((rows,...  140 us

profile of v6, /device:TPU:112, one launch (start us, length us, event | category | flops | bytes accessed | tf_op | source)
XLA Modules:
  0.0 141.6 jit_solution(1019329458242070849)
XLA Ops:
  0.0 140.3 %shard_map.46 = bf16[512,2048]{1,0:T(8,128)(2,1)S(1)} custom-call(bf16[512,2048]{1,0:T(8,128)(2,1)} %x_hbm.1, bf16[2048,1024]{1,0:T(8,128)(2,1)} %wg_hbm.1, bf16[2048,1024]{1,0:T(8,128)(2,1)} %wu_hbm.1, bf16[1024,2048]{1,0:T(8,128)(2,1)} %wd_hbm.1), custom_call_target="tpu_custom_call" | custom-call | tf_op jit(solution)/shard_map/pallas_call | solution.py:248
  140.3 1.3 copy.6

commit v7 on v6

--- a/solution.py
+++ b/solution.py
@@ -92,11 +92,17 @@
         for src, dst in ((wg_hbm, wg), (wu_hbm, wu), (wd_hbm, wd))
     ]
     barrier = pltpu.get_barrier_semaphore()
-    for device in (partner, right, left):
+
+    def greet(device):
         pl.semaphore_signal(barrier, inc=1, device_id=device, device_id_type=pl.DeviceIdType.MESH)
+
+    core = lax.rem(me, CORES)
+    greet(right)
+    greet(left)
     for c in own + weights:
         c.start()
-    pl.semaphore_wait(barrier, 3)
+    pl.semaphore_wait(barrier, 3 - core)
+    greet(partner)
     for h in range(2):
         gather(2 + h, 0, x_hbm.at[pl.ds(h * half, FIRST)]).start()
     for h in range(2):
@@ -104,6 +110,11 @@
     for h in range(2):
         own[2 + h].wait()
         gather(2 + h, 1).start()
+
+    @pl.when(core == 1)
+    def _():
+        pl.semaphore_wait(barrier, 1)
+
     for h in range(2):
         relay(h).start()
     def arrive_near(p):

time: 142 us -> 141 us (level)
  no operation moved by 1% of the time
where the time goes in v7:
time: 141 us
  Pallas kernels  140 us (99%)
    pallas_call x1, Pallas kernels, step(): pl.pallas_call(functools.partial(kernel, n), out_shape=pltpu.VMEM((rows,...  140 us

profile of v7, /device:TPU:112, one launch (start us, length us, event | category | flops | bytes accessed | tf_op | source)
XLA Modules:
  0.0 141.4 jit_solution(161056666802024786)
XLA Ops:
  0.0 140.1 %shard_map.46 = bf16[512,2048]{1,0:T(8,128)(2,1)S(1)} custom-call(bf16[512,2048]{1,0:T(8,128)(2,1)} %x_hbm.1, bf16[2048,1024]{1,0:T(8,128)(2,1)} %wg_hbm.1, bf16[2048,1024]{1,0:T(8,128)(2,1)} %wu_hbm.1, bf16[1024,2048]{1,0:T(8,128)(2,1)} %wd_hbm.1), custom_call_target="tpu_custom_call" | custom-call | tf_op jit(solution)/shard_map/pallas_call | solution.py:259
  140.1 1.3 copy.6

commit v8 on v7

--- a/solution.py
+++ b/solution.py
@@ -21,7 +21,7 @@
 def kernel(
     n, x_hbm, wg_hbm, wu_hbm, wd_hbm, y_ref,
     x_all, wg, wu, wd, hidden, acc, terms, partner_terms, arrived,
-    own_sem, weight_sem, ring_send, partner_send, near_recv, half_recv, relay_recv, pt_recv,
+    hello, own_sem, weight_sem, ring_send, partner_send, near_recv, half_recv, relay_recv, pt_recv,
 ):
     half, depth = x_all.shape[1:]
     me = lax.axis_index("tp")
@@ -97,14 +97,17 @@
         pl.semaphore_signal(barrier, inc=1, device_id=device, device_id_type=pl.DeviceIdType.MESH)
 
     core = lax.rem(me, CORES)
-    greet(right)
     greet(left)
     for c in own + weights:
         c.start()
-    pl.semaphore_wait(barrier, 3 - core)
-    greet(partner)
-    for h in range(2):
+    pl.semaphore_wait(barrier, 2 - core)
+    pl.semaphore_signal(hello, inc=1, device_id=right, device_id_type=pl.DeviceIdType.MESH)
+    for h in range(2):
+        if h == 1:
+            pl.semaphore_wait(hello, 1)
         gather(2 + h, 0, x_hbm.at[pl.ds(h * half, FIRST)]).start()
+        if h == 0:
+            greet(partner)
     for h in range(2):
         own[h].wait()
     for h in range(2):
@@ -271,6 +274,7 @@
                 pltpu.VMEM((6, half, depth), bf16),
                 pltpu.VMEM((SLOTS, half, depth), bf16),
                 pltpu.VMEM((6, half, depth), bf16),
+                pltpu.SemaphoreType.REGULAR,
                 dma((2, 2)),
                 dma((1,)),
                 dma((1,)),

time: 141 us -> 141 us (level)
  no operation moved by 1% of the time
where the time goes in v8:
time: 141 us
  Pallas kernels  140 us (99%)
    pallas_call x1, Pallas kernels, step(): pl.pallas_call(functools.partial(kernel, n), out_shape=pltpu.VMEM((rows,...  140 us

profile of v8, /device:TPU:112, one launch (start us, length us, event | category | flops | bytes accessed | tf_op | source)
XLA Modules:
  0.0 141.0 jit_solution(4411791539880844805)
XLA Ops:
  0.0 139.7 %shard_map.46 = bf16[512,2048]{1,0:T(8,128)(2,1)S(1)} custom-call(bf16[512,2048]{1,0:T(8,128)(2,1)} %x_hbm.1, bf16[2048,1024]{1,0:T(8,128)(2,1)} %wg_hbm.1, bf16[2048,1024]{1,0:T(8,128)(2,1)} %wu_hbm.1, bf16[1024,2048]{1,0:T(8,128)(2,1)} %wd_hbm.1), custom_call_target="tpu_custom_call" | custom-call | tf_op jit(solution)/shard_map/pallas_call | solution.py:262
  139.7 1.3 copy.6

commit v9 on v8

--- a/solution.py
+++ b/solution.py
@@ -98,16 +98,14 @@
 
     core = lax.rem(me, CORES)
     greet(left)
+    pl.semaphore_wait(barrier, 2 - core)
+    gather(2, 0, x_hbm.at[pl.ds(0, FIRST)]).start()
+    pl.semaphore_signal(hello, inc=1, device_id=right, device_id_type=pl.DeviceIdType.MESH)
+    greet(partner)
     for c in own + weights:
         c.start()
-    pl.semaphore_wait(barrier, 2 - core)
-    pl.semaphore_signal(hello, inc=1, device_id=right, device_id_type=pl.DeviceIdType.MESH)
-    for h in range(2):
-        if h == 1:
-            pl.semaphore_wait(hello, 1)
-        gather(2 + h, 0, x_hbm.at[pl.ds(h * half, FIRST)]).start()
-        if h == 0:
-            greet(partner)
+    pl.semaphore_wait(hello, 1)
+    gather(3, 0, x_hbm.at[pl.ds(half, FIRST)]).start()
     for h in range(2):
         own[h].wait()
     for h in range(2):

time: 141 us -> 141 us (level)
  no operation moved by 1% of the time
where the time goes in v9:
time: 141 us
  Pallas kernels  140 us (99%)
    pallas_call x1, Pallas kernels, step(): pl.pallas_call(functools.partial(kernel, n), out_shape=pltpu.VMEM((rows,...  140 us

profile of v9, /device:TPU:112, one launch (start us, length us, event | category | flops | bytes accessed | tf_op | source)
XLA Modules:
  0.0 141.0 jit_solution(13733811694840194170)
XLA Ops:
  0.0 139.7 %shard_map.46 = bf16[512,2048]{1,0:T(8,128)(2,1)S(1)} custom-call(bf16[512,2048]{1,0:T(8,128)(2,1)} %x_hbm.1, bf16[2048,1024]{1,0:T(8,128)(2,1)} %wg_hbm.1, bf16[2048,1024]{1,0:T(8,128)(2,1)} %wu_hbm.1, bf16[1024,2048]{1,0:T(8,128)(2,1)} %wd_hbm.1), custom_call_target="tpu_custom_call" | custom-call | tf_op jit(solution)/shard_map/pallas_call | solution.py:260
  139.7 1.3 copy.6
